TPU v7x, 256 devices: a whole 4x4x8 slice. The times are simulated.
256 devices in a mesh: row: 8 (over x, core), col: 32 (over y, z).
Axes of the slice: x: 4, y: 4, z: 8, core: 2. Of those that a mesh axis runs over, the one named last changes fastest.
Arguments:
- pooled: bfloat16 [16384, 1152], P(('row', 'col')), may hold values from -32 to 32
- hidden: bfloat16 [16384, 4304], P(('row', 'col')), may hold values from -6 to 6
- text: bfloat16 [16384, 1152], P(('row', 'col')), may hold values from -12 to 12
- weight: float32 [1152, 4304], P('col', 'row'), may hold values from -0.09375 to 0.09375
- row_moment: float32 [1152], P('col'), may hold values from 1e-07 to 1e-05
- col_moment: float32 [4304], P('row'), may hold values from 1e-07 to 1e-05
- log_scale: float32 [], replicated, may hold values from 4.2 to 4.8
- bias: float32 [], replicated, may hold values from -16 to -12
Outputs:
- update: float32 [1152, 4304], P('col', 'row')
- new_row: float32 [1152], P('col')
- new_col: float32 [4304], P('row')
- loss: float32 [], replicated
All inputs are finite; a program needn't handle non-finite values.
Results may differ from a plain program's by a relative error of at most 0.004.
Values may be sent and summed in bfloat16 or wider, within the bound.
No kernel may reach another device: no remote copies, remote signals or barrier semaphores. Data moves between devices by JAX's collectives and lax.ppermute only.
A program may use at most 128 MiB of HBM per device.

v0:
```python
import functools
import jax
import jax.numpy as jnp
from jax import lax
from jax.sharding import Mesh
from jax.sharding import PartitionSpec as P

D = 1152
FF = 4304
ROW = ("row_0", "row_1")
COL = ("col_0", "col_1")
ROW_COL = ("row_0", "row_1", "col_0", "col_1")
EPSILON = 1e-06
DECAY_RATE = 0.8
CLIP_LEVEL = 1.0
FLOOR_VALUE = 1e-30


def laid_out(pieces, dim):
    dims = list(pieces.shape[1:])
    dims[dim] *= pieces.shape[0]
    return jnp.moveaxis(pieces, 0, dim).reshape(dims)


def sent_to_all(array, axis):
    copies = jnp.broadcast_to(array, (lax.axis_size(axis), *array.shape))
    return lax.all_to_all(copies, axis, split_axis=0, concat_axis=0, tiled=True)


def collect(array, axis, dim):
    return laid_out(sent_to_all(array, axis), dim)


def split_up(array, dim, devices):
    dims = array.shape
    pieces = array.reshape(*dims[:dim], devices, dims[dim] // devices, *dims[dim + 1 :])
    return jnp.moveaxis(pieces, dim, 0)


def sum_at_owner(array, axis, dim):
    pieces = split_up(array, dim, lax.axis_size(axis))
    arrived = lax.all_to_all(pieces, axis, split_axis=0, concat_axis=0, tiled=True)
    return arrived.sum(axis=0)


def sum_by_axis(running, axes):
    for axis in axes:
        running = lax.psum_scatter(running, axis, scatter_dimension=0, tiled=True)
    return running


def of_everyone(array, axis):
    everything = sent_to_all(array, axis)
    return jnp.sum(everything, axis=0)


def one_axis_at_a_time(array, axes):
    return functools.reduce(lax.psum, axes, array)


def over_row_index(positions, column, tokens, columns):
    return (positions // tokens * columns + column) * tokens + positions % tokens


def over_col_index(positions, row_place, tokens, columns):
    return row_place * columns * tokens + positions


def pair_tile(images, image_ids, texts, text_ids, logit_scale, bias, batch_total):
    logits = logit_scale * jnp.dot(images, texts.T, preferred_element_type=jnp.float32) + bias
    label_sign = jnp.where(
        image_ids[:, None] == text_ids[None, :], jnp.float32(1.0), jnp.float32(-1.0)
    )
    loss_sum = jnp.sum(jax.nn.softplus(-label_sign * logits))
    grad_logits = (-label_sign * jax.nn.sigmoid(-label_sign * logits) / batch_total).astype(
        jnp.bfloat16
    )
    return (loss_sum, logit_scale * jnp.dot(grad_logits, texts, preferred_element_type=jnp.float32))


def per_device(pooled, hidden, text, weight, row_moment, col_moment, log_scale, bias):
    rows_count = lax.axis_size(ROW)
    cols_count = lax.axis_size(COL)
    row_place = lax.axis_index(ROW)
    col_place = lax.axis_index(COL)
    tokens = pooled.shape[0]
    batch_total = tokens * rows_count * cols_count
    split_hidden = lax.all_to_all(hidden, ROW, split_axis=1, concat_axis=0, tiled=True)
    weight_half = weight.astype(jnp.bfloat16)
    partial_proj = lax.dot_general(
        split_hidden,
        collect(weight_half, COL, 0),
        (((1,), (1,)), ((), ())),
        preferred_element_type=jnp.float32,
    )
    projected = sum_at_owner(partial_proj, ROW, 0)
    mixed_rows = pooled.astype(jnp.float32) + projected
    length = jnp.sqrt(jnp.sum(mixed_rows * mixed_rows, axis=1, keepdims=True) + EPSILON)
    image_unit = mixed_rows / length
    images = image_unit.astype(jnp.bfloat16)
    text_float = text.astype(jnp.float32)
    text_units = (
        text_float / jnp.sqrt(jnp.sum(text_float * text_float, axis=1, keepdims=True) + EPSILON)
    ).astype(jnp.bfloat16)
    logit_scale = jnp.exp(log_scale)
    image_rows = collect(images, ROW, 0)
    image_ids = over_row_index(
        jnp.arange(image_rows.shape[0], dtype=jnp.int32), col_place, tokens, cols_count
    )
    piece = lax.all_gather(text_units, COL, axis=0, tiled=True)
    text_ids = over_col_index(
        jnp.arange(piece.shape[0], dtype=jnp.int32), row_place, tokens, cols_count
    )
    loss_local, unit_part = pair_tile(
        image_rows, image_ids, piece, text_ids, logit_scale, bias, batch_total
    )
    unit_grad = sum_at_owner(unit_part, ROW, 0)
    mixed_grad = (
        (unit_grad - image_unit * jnp.sum(image_unit * unit_grad, axis=1, keepdims=True)) / length
    ).astype(jnp.bfloat16)
    grad_rows = collect(mixed_grad, ROW, 0)
    gradient = sum_by_axis(
        lax.dot_general(
            grad_rows, split_hidden, (((0,), (0,)), ((), ())), preferred_element_type=jnp.float32
        ),
        COL,
    )
    squared = gradient * gradient + FLOOR_VALUE
    row_sum = of_everyone(jnp.sum(squared, axis=1), ROW)
    col_sum = of_everyone(jnp.sum(squared, axis=0), COL)
    new_row = DECAY_RATE * row_moment + (1.0 - DECAY_RATE) * row_sum / FF
    new_col = DECAY_RATE * col_moment + (1.0 - DECAY_RATE) * col_sum / D
    second = new_row[:, None] * new_col[None, :]
    raw_update = gradient / jnp.sqrt(second)
    loss_total, update_total = (
        one_axis_at_a_time(loss_local, ROW_COL),
        one_axis_at_a_time(jnp.sum(raw_update * raw_update), ROW_COL),
    )
    update_rms = jnp.sqrt(update_total / (D * FF))
    update = raw_update / jnp.maximum(1.0, update_rms / CLIP_LEVEL)
    loss = loss_total / batch_total
    return (update, new_row, new_col, loss)


def solution(mesh):
    finer = Mesh(mesh.devices.reshape(4, 2, 4, 8), ("row_0", "row_1", "col_0", "col_1"))
    return jax.shard_map(
        per_device,
        mesh=finer,
        in_specs=(
            P(ROW_COL, None),
            P(ROW_COL, None),
            P(ROW_COL, None),
            P(COL, ROW),
            P(COL),
            P(ROW),
            P(),
            P(),
        ),
        out_specs=(P(COL, ROW), P(COL), P(ROW), P()),
        check_vma=False,
    )
```

profile of v0, /device:TPU:2, one launch (start us, length us, event | category | flops | bytes accessed | tf_op | source)
XLA Modules:
  0.0 357.6 jit_solution(11246897454921141489)
XLA Ops:
  7.2 1.1 fusion.10
  8.3 1.7 fusion.11
  10.0 0.9 convert_element_type.22
  10.9 1.3 broadcast_in_dim.32
  12.2 11.5 %all-to-all-start.1 = ((bf16[32,36,538]{2,1,0:T(8,128)(2,1)}), bf16[32,36,538]{2,1,0:T(8,128)(2,1)S(1)}, u32[]{:S(2)}, u32[]{:S(2)}) async-start(bf16[32,36,538]{2,1,0:T(8,128)(2,1)} %broadcast_in_dim.32), calls=%async_computation.1 | async-start | bytes 3276800 | tf_op jit(solution)/shard_map/all_to_all | solution.py:27
  23.8 0.8 all_to_all.35
  24.5 0.9 copy.19
  25.5 44.5 %all-to-all-done.1 = bf16[32,36,538]{2,1,0:T(8,128)(2,1)S(1)} async-done(((bf16[32,36,538]{2,1,0:T(8,128)(2,1)}), bf16[32,36,538]{2,1,0:T(8,128)(2,1)S(1)}, u32[]{:S(2)}, u32[]{:S(2)}) %all-to-all-start.1) | async-done | bytes 1239584 | tf_op jit(solution)/shard_map/all_to_all | solution.py:27
  69.9 4.8 %all-to-all-start = ((bf16[64,8,538]{2,0,1:T(8,128)(2,1)}), bf16[64,8,538]{2,0,1:T(8,128)(2,1)}, u32[]{:S(2)}, u32[]{:S(2)}) async-start(bf16[64,8,538]{2,0,1:T(8,128)(2,1)} %copy.19), calls=%async_computation | async-start | bytes 1310720 | tf_op jit(solution)/shard_map/all_to_all | solution.py:88
  75.4 9.7 %all-to-all-done = bf16[64,8,538]{2,0,1:T(8,128)(2,1)} async-done(((bf16[64,8,538]{2,0,1:T(8,128)(2,1)}), bf16[64,8,538]{2,0,1:T(8,128)(2,1)}, u32[]{:S(2)}, u32[]{:S(2)}) %all-to-all-start) | async-done | bytes 550944 | tf_op jit(solution)/shard_map/all_to_all | solution.py:88
  85.1 2.3 fusion.6
  87.5 32.9 %all_to_all.53 = f32[8,64,1152]{2,1,0:T(8,128)S(1)} all-to-all(f32[8,64,1152]{2,1,0:T(8,128)S(1)} %fusion.6), channel_id=1, replica_groups=mesh['row_0'=4,'row_1'=2,'col_0'=4,'col_1'=8] {'row_0','row_1'}, dimensions={0} | all-to-all | bytes 4718592 | tf_op jit(solution)/shard_map/all_to_all | solution.py:42
  120.8 1.2 broadcast_in_dim.33
  122.0 4.7 %all-to-all-start.3 = ((bf16[8,64,1152]{2,1,0:T(8,128)(2,1)}), bf16[8,64,1152]{2,1,0:T(8,128)(2,1)S(1)}, u32[]{:S(2)}, u32[]{:S(2)}) async-start(bf16[8,64,1152]{2,1,0:T(8,128)(2,1)} %broadcast_in_dim.33), calls=%async_computation.3 | async-start | bytes 2359296 | tf_op jit(solution)/shard_map/all_to_all | solution.py:27
  128.0 14.5 %all-to-all-done.3 = bf16[8,64,1152]{2,1,0:T(8,128)(2,1)S(1)} async-done(((bf16[8,64,1152]{2,1,0:T(8,128)(2,1)}), bf16[8,64,1152]{2,1,0:T(8,128)(2,1)S(1)}, u32[]{:S(2)}, u32[]{:S(2)}) %all-to-all-start.3) | async-done | bytes 1179680 | tf_op jit(solution)/shard_map/all_to_all | solution.py:27
  142.5 8.2 %fusion.1 = (f32[]{:T(128)}, f32[512,2048]{1,0:T(8,128)S(1)}) fusion(f32[]{:T(128)S(6)} %copy.27, bf16[512,1152]{1,0:T(8,128)(2,1)S(1)} %bitcast.21, bf16[2048,1152]{1,0:T(8,128)(2,1)} %all-gather.2.cloned.1.call-done, f32[]{:T(128)S(6)} %exp.10, s32[2048]{0:T(1024)S(1)} %iota_add_fusion, s32[512]{0:T(512)S(1)} %fusion.23), kind=kOutput, calls=%fused_computation.1 | convolution fusion | flops 2429550592 | bytes 10102796 | tf_op jit(solution)/shard_map/dot_general | solution.py:70
  150.8 3.7 %convolution_multiply_fusion = f32[512,1152]{1,0:T(8,128)S(1)} fusion(bf16[2048,1152]{1,0:T(8,128)(2,1)S(1)} %copy-done.6, f32[512,2048]{1,0:T(8,128)S(1)} %get-tuple-element.15, s32[2048]{0:T(1024)S(1)} %iota_add_fusion, s32[512]{0:T(512)S(1)} %fusion.23, f32[]{:T(128)S(6)} %exp.10), kind=kOutput, calls=%fused_computation.6 | convolution fusion | flops 2425946112 | bytes 11282436 | tf_op jit(solution)/shard_map/dot_general | solution.py:78
  154.5 32.7 %all_to_all.54 = f32[8,64,1152]{2,1,0:T(8,128)S(1)} all-to-all(f32[8,64,1152]{2,1,0:T(8,128)S(1)} %bitcast.20), channel_id=1, replica_groups=mesh['row_0'=4,'row_1'=2,'col_0'=4,'col_1'=8] {'row_0','row_1'}, dimensions={0} | all-to-all | bytes 4718592 | tf_op jit(solution)/shard_map/all_to_all | solution.py:42
  187.8 19.6 %all_to_all.55 = bf16[8,64,1152]{2,1,0:T(8,128)(2,1)S(1)} all-to-all(bf16[8,64,1152]{2,1,0:T(8,128)(2,1)S(1)} %broadcast_in_dim.34), channel_id=1, replica_groups=mesh['row_0'=4,'row_1'=2,'col_0'=4,'col_1'=8] {'row_0','row_1'}, dimensions={0} | all-to-all | bytes 2359296 | tf_op jit(solution)/shard_map/all_to_all | solution.py:27
  207.4 3.8 %convolution_bitcast_fusion = f32[1152,538]{1,0:T(8,128)} fusion(bf16[8,64,1152]{2,1,0:T(8,128)(2,1)S(1)} %all_to_all.55, bf16[64,8,538]{2,0,1:T(8,128)(2,1)} %all-to-all-done), kind=kOutput, calls=%fused_computation.5 | convolution fusion | flops 634650624 | bytes 4209664 | tf_op jit(solution)/shard_map/dot_general | solution.py:123
  211.2 35.5 %reduce-scatter.4.cloned.1.call-done = f32[288,538]{1,0:T(8,128)} async-done(((f32[1152,538]{1,0:T(8,128)}), f32[288,538]{1,0:T(8,128)}) %reduce-scatter.4.cloned.1.call-update) | async-done | bytes 619792 | tf_op jit(solution)/shard_map/reduce_scatter | solution.py:48
  246.7 23.8 %fusion = f32[48,538]{1,0:T(8,128)S(1)} fusion(f32[288,538]{1,0:T(8,128)} %reduce-scatter.4.cloned.1.call-done), kind=kCustom, calls=%all-reduce-scatter | all-reduce-scatter fusion | flops 206593 | bytes 724096
  270.5 2.8 collective-permute-start
  273.3 2.4 collective-permute-start.1
  277.0 1.0 collective-permute-done.1
  278.5 8.4 %all_to_all.56 = f32[8,1,36]{2,1,0:T(1,128)S(1)} all-to-all(f32[8,1,36]{2,1,0:T(1,128)S(1)} %broadcast_in_dim.35), channel_id=1, replica_groups=mesh['row_0'=4,'row_1'=2,'col_0'=4,'col_1'=8] {'row_0','row_1'}, dimensions={0} | all-to-all | bytes 2304 | tf_op jit(solution)/shard_map/all_to_all | solution.py:27
  287.6 10.9 %all-to-all-start.7 = ((f32[32,1,538]{2,1,0:T(1,128)}), f32[32,1,538]{2,1,0:T(1,128)S(1)}, u32[]{:S(2)}, u32[]{:S(2)}) async-start(f32[32,1,538]{2,1,0:T(1,128)} %broadcast_in_dim.36), calls=%async_computation.8 | async-start | bytes 163840 | tf_op jit(solution)/shard_map/all_to_all | solution.py:27
  298.6 10.0 %all-to-all-done.7 = f32[32,1,538]{2,1,0:T(1,128)S(1)} async-done(((f32[32,1,538]{2,1,0:T(1,128)}), f32[32,1,538]{2,1,0:T(1,128)S(1)}, u32[]{:S(2)}, u32[]{:S(2)}) %all-to-all-start.7) | async-done | bytes 68896 | tf_op jit(solution)/shard_map/all_to_all | solution.py:27
  309.4 9.8 %all-reduce.4 = (f32[]{:T(128)}, f32[]{:T(128)}) all-reduce(f32[]{:T(128)} %multiply_reduce_fusion.2, f32[]{:T(128)} %get-tuple-element.14), channel_id=1, replica_groups=mesh['row_0'=4,'row_1'=2,'col_0'=4,'col_1'=8] {'row_0'}, use_global_device_ids=true, to_apply=%region_12.13 | all-reduce | flops 2 | bytes 16 | tf_op jit(solution)/shard_map/psum | solution.py:58
  319.2 3.1 all-reduce.5
  322.3 9.5 %all-reduce.3 = (f32[]{:T(128)}, f32[]{:T(128)}) all-reduce(f32[]{:T(128)} %get-tuple-element.12, f32[]{:T(128)} %get-tuple-element.13), channel_id=1, replica_groups=mesh['row_0'=4,'row_1'=2,'col_0'=4,'col_1'=8] {'col_0'}, use_global_device_ids=true, to_apply=%region_14.15 | all-reduce | flops 2 | bytes 16 | tf_op jit(solution)/shard_map/psum | solution.py:58
  331.8 15.7 %all-reduce.2 = (f32[]{:T(128)}, f32[]{:T(128)}) all-reduce(f32[]{:T(128)} %get-tuple-element.8, f32[]{:T(128)} %get-tuple-element.9), channel_id=1, replica_groups=mesh['row_0'=4,'row_1'=2,'col_0'=4,'col_1'=8] {'col_1'}, use_global_device_ids=true, to_apply=%region_15.16 | all-reduce | flops 2 | bytes 16 | tf_op jit(solution)/shard_map/psum | solution.py:58
  (46 shorter events, 5.1 us)
Async XLA Ops:
  7.2 16.6 %copy-start.1 = (bf16[64,4304]{1,0:T(8,128)(2,1)S(1)}, bf16[64,4304]{1,0:T(8,128)(2,1)}, u32[]{:S(2)}) copy-start(bf16[64,4304]{1,0:T(8,128)(2,1)} %param.9) | copy-start | bytes 1652740
  7.2 135.4 %all-gather.2.cloned.1.call-start = ((), (), s32[]{:S(2)}) async-start(), calls=%async_computation.9 | async-start | bytes 4866048 | tf_op jit(solution)/shard_map/all_gather | solution.py:110
  12.2 57.7 %all-to-all-start.1 = ((bf16[32,36,538]{2,1,0:T(8,128)(2,1)}), bf16[32,36,538]{2,1,0:T(8,128)(2,1)S(1)}, u32[]{:S(2)}, u32[]{:S(2)}) async-start(bf16[32,36,538]{2,1,0:T(8,128)(2,1)} %broadcast_in_dim.32), calls=%async_computation.1 | async-start | bytes 3276800 | tf_op jit(solution)/shard_map/all_to_all | solution.py:27
  69.9 15.2 %all-to-all-start = ((bf16[64,8,538]{2,0,1:T(8,128)(2,1)}), bf16[64,8,538]{2,0,1:T(8,128)(2,1)}, u32[]{:S(2)}, u32[]{:S(2)}) async-start(bf16[64,8,538]{2,0,1:T(8,128)(2,1)} %copy.19), calls=%async_computation | async-start | bytes 1310720 | tf_op jit(solution)/shard_map/all_to_all | solution.py:88
  87.4 33.1 %copy-start = (bf16[64,1152]{1,0:T(8,128)(2,1)S(1)}, bf16[64,1152]{1,0:T(8,128)(2,1)}, u32[]{:S(2)}) copy-start(bf16[64,1152]{1,0:T(8,128)(2,1)} %param.8) | copy-start | bytes 442372
  122.0 20.6 %all-to-all-start.3 = ((bf16[8,64,1152]{2,1,0:T(8,128)(2,1)}), bf16[8,64,1152]{2,1,0:T(8,128)(2,1)S(1)}, u32[]{:S(2)}, u32[]{:S(2)}) async-start(bf16[8,64,1152]{2,1,0:T(8,128)(2,1)} %broadcast_in_dim.33), calls=%async_computation.3 | async-start | bytes 2359296 | tf_op jit(solution)/shard_map/all_to_all | solution.py:27
  126.6 120.1 %reduce-scatter.4.cloned.1.call-start = ((), (), s32[]{:S(2)}) async-start(), calls=%async_computation.10 | async-start | bytes 3686400 | tf_op jit(solution)/shard_map/reduce_scatter | solution.py:48
  142.5 8.2 %copy-start.6 = (bf16[2048,1152]{1,0:T(8,128)(2,1)S(1)}, bf16[2048,1152]{1,0:T(8,128)(2,1)}, u32[]{:S(2)}) copy-start(bf16[2048,1152]{1,0:T(8,128)(2,1)} %all-gather.2.cloned.1.call-done) | copy-start | bytes 14155780
  207.4 68.3 %copy-start.5 = (u32[256]{0:T(256)S(1)}, u32[256]{0:T(256)}, u32[]{:S(2)}) copy-start(u32[256]{0:T(256)} %constant.101) | copy-start | bytes 3076
  211.2 87.3 %copy-start.7 = (f32[36]{0:T(128)S(1)}, f32[36]{0:T(128)}, u32[]{:S(2)}) copy-start(f32[36]{0:T(128)} %param.12) | copy-start | bytes 436
  211.2 97.4 %copy-start.3 = (f32[538]{0:T(1024)S(1)}, f32[538]{0:T(1024)}, u32[]{:S(2)}) copy-start(f32[538]{0:T(1024)} %param.13) | copy-start | bytes 6460
  270.5 7.5 %collective-permute-start = (f32[48,538]{1,0:T(8,128)S(1)}, f32[48,538]{1,0:T(8,128)S(1)}, u32[]{:S(2)}, u32[]{:S(2)}) collective-permute-start(f32[48,538]{1,0:T(8,128)S(1)} %fusion), channel_id=1, source_target_pairs={{0,1},{1,2},{2,3},{3,4},{4,5},{5,6},{6,7},{8,9},{9,10},{10,11},{11... | collective-permute-start | bytes 309896
  273.3 4.6 %collective-permute-start.1 = (f32[36,538]{1,0:T(8,128)S(1)}, f32[36,538]{1,0:T(8,128)S(1)}, u32[]{:S(2)}, u32[]{:S(2)}) collective-permute-start(f32[36,538]{1,0:T(8,128)S(1)} %slice), channel_id=1, source_target_pairs={{0,2},{1,3},{2,4},{3,5},{4,6},{5,7},{8,10},{9,11},{10,12},{11,13},... | collective-permute-start | bytes 232424
  287.6 21.0 %all-to-all-start.7 = ((f32[32,1,538]{2,1,0:T(1,128)}), f32[32,1,538]{2,1,0:T(1,128)S(1)}, u32[]{:S(2)}, u32[]{:S(2)}) async-start(f32[32,1,538]{2,1,0:T(1,128)} %broadcast_in_dim.36), calls=%async_computation.8 | async-start | bytes 163840 | tf_op jit(solution)/shard_map/all_to_all | solution.py:27
  298.6 51.0 %copy-start.4 = (f32[36]{0:T(128)}, f32[36]{0:T(128)S(1)}, u32[]{:S(2)}) copy-start(f32[36]{0:T(128)S(1)} %multiply_add_fusion.2) | copy-start | bytes 436
  308.7 40.9 %copy-start.2 = (f32[538]{0:T(1024)}, f32[538]{0:T(1024)S(1)}, u32[]{:S(2)}) copy-start(f32[538]{0:T(1024)S(1)} %multiply_add_fusion.1) | copy-start | bytes 6460
Sparse Core Ops, SparseCore 0:
  10.6 92.3 all-gather.1
  211.4 35.3 reduce-scatter.3
where the time goes:
time: 358 us
  blocking collectives  156 us (44%)
  waiting for transfers between devices  115 us (32%)
  starting transfers between devices  37.1 us (10%)
  between operations  18.7 us (5%)
  matrix products  18 us (5%)
  local copies, waits for them, and re-layouts  6.69 us (2%)
  other arithmetic  6.23 us (2%)
    all_to_all x3, waiting for transfers between devices, sent_to_all(): return lax.all_to_all(copies, axis, split_axis=0, concat_axis=0, tiled=True)  69 us
    all_to_all x2, blocking collectives, sum_at_owner(): lax.all_to_all(pieces, axis, split_axis=0, concat_axis=0, tiled=True)  65.6 us
    psum x4, blocking collectives, one_axis_at_a_time(): return functools.reduce(lax.psum, axes, array)  38.1 us
    reduce_scatter x1, waiting for transfers between devices, sum_by_axis(): running = lax.psum_scatter(running, axis, scatter_dimension=0, tiled=True)  35.5 us
    all_to_all x2, blocking collectives, sent_to_all(): return lax.all_to_all(copies, axis, split_axis=0, concat_axis=0, tiled=True)  28 us
    all_to_all x3, starting transfers between devices, sent_to_all(): return lax.all_to_all(copies, axis, split_axis=0, concat_axis=0, tiled=True)  27.1 us
    unnamed x1, blocking collectives  23.8 us
    all_to_all x1, waiting for transfers between devices, per_device(): lax.all_to_all(hidden, ROW, split_axis=1, concat_axis=0, tiled=True)  9.71 us
  transfers between devices with their start and end apart: 8, of which 6 were waited for; matrix products, arithmetic and copies ran while one was open for 2% of the time, Pallas kernels for 0%

commit v1 on v0

--- a/solution.py
+++ b/solution.py
@@ -85,7 +85,9 @@
     col_place = lax.axis_index(COL)
     tokens = pooled.shape[0]
     batch_total = tokens * rows_count * cols_count
-    split_hidden = lax.all_to_all(hidden, ROW, split_axis=1, concat_axis=0, tiled=True)
+    split_hidden = jnp.concatenate(
+        lax.all_to_all(jnp.stack(jnp.split(hidden, lax.axis_size(ROW), axis=1)), ROW, 0, 0), axis=0
+    )
     weight_half = weight.astype(jnp.bfloat16)
     partial_proj = lax.dot_general(
         split_hidden,

time: 358 us -> 358 us (level)
  local copies, waits for them, and re-layouts: 6.69 us -> 10.7 us
  waiting for transfers between devices: 115 us -> 111 us
    unnamed x19 -> x26, local copies, waits for them, and re-layouts: 1.01 us -> 5.99 us
    all_to_all x3, waiting for transfers between devices: 69 us -> 65 us  [sent_to_all(): return lax.all_to_all(copies, axis, split_axis=0, concat_axis=0, tiled=True)]
  transfers between devices with their start and end apart: 8 -> 8, of which waited for: 6 -> 6; matrix products, arithmetic and copies ran while one was open for 2% -> 4% of each run, Pallas kernels for 0% -> 0%
where the time goes in v1:
time: 358 us
  blocking collectives  156 us (44%)
  waiting for transfers between devices  111 us (31%)
  starting transfers between devices  37.1 us (10%)
  between operations  18.7 us (5%)
  matrix products  18 us (5%)
  local copies, waits for them, and re-layouts  10.7 us (3%)
  other arithmetic  6.23 us (2%)
    all_to_all x2, blocking collectives, sum_at_owner(): lax.all_to_all(pieces, axis, split_axis=0, concat_axis=0, tiled=True)  65.6 us
    all_to_all x3, waiting for transfers between devices, sent_to_all(): return lax.all_to_all(copies, axis, split_axis=0, concat_axis=0, tiled=True)  65 us
    psum x4, blocking collectives, one_axis_at_a_time(): return functools.reduce(lax.psum, axes, array)  38.1 us
    reduce_scatter x1, waiting for transfers between devices, sum_by_axis(): running = lax.psum_scatter(running, axis, scatter_dimension=0, tiled=True)  35.5 us
    all_to_all x2, blocking collectives, sent_to_all(): return lax.all_to_all(copies, axis, split_axis=0, concat_axis=0, tiled=True)  28.1 us
    all_to_all x3, starting transfers between devices, sent_to_all(): return lax.all_to_all(copies, axis, split_axis=0, concat_axis=0, tiled=True)  27 us
    unnamed x1, blocking collectives  23.7 us
    all_to_all x1, waiting for transfers between devices, per_device(): lax.all_to_all(jnp.stack(jnp.split(hidden, lax.axis_size(ROW), axis=1)),...  9.71 us
  transfers between devices with their start and end apart: 8, of which 6 were waited for; matrix products, arithmetic and copies ran while one was open for 4% of the time, Pallas kernels for 0%

profile of v1, /device:TPU:2, one launch (start us, length us, event | category | flops | bytes accessed | tf_op | source)
XLA Modules:
  0.0 357.6 jit_solution(7524342107053118465)
XLA Ops:
  7.2 1.1 fusion.8
  8.3 1.7 fusion.9
  10.0 0.9 convert_element_type.22
  10.9 1.3 broadcast_in_dim.32
  12.2 11.5 %all-to-all-start.1 = ((bf16[32,36,538]{2,1,0:T(8,128)(2,1)}), bf16[32,36,538]{2,1,0:T(8,128)(2,1)S(1)}, u32[]{:S(2)}, u32[]{:S(2)}) async-start(bf16[32,36,538]{2,1,0:T(8,128)(2,1)} %broadcast_in_dim.32), calls=%async_computation.1 | async-start | bytes 3276800 | tf_op jit(solution)/shard_map/all_to_all | solution.py:27
  26.6 0.7 bitcast_dynamic-update-slice_fusion.3
  29.5 40.5 %all-to-all-done.1 = bf16[32,36,538]{2,1,0:T(8,128)(2,1)S(1)} async-done(((bf16[32,36,538]{2,1,0:T(8,128)(2,1)}), bf16[32,36,538]{2,1,0:T(8,128)(2,1)S(1)}, u32[]{:S(2)}, u32[]{:S(2)}) %all-to-all-start.1) | async-done | bytes 1239584 | tf_op jit(solution)/shard_map/all_to_all | solution.py:27
  69.9 4.8 %all-to-all-start = ((bf16[8,64,538]{2,1,0:T(8,128)(2,1)}), bf16[8,64,538]{2,1,0:T(8,128)(2,1)}, u32[]{:S(2)}, u32[]{:S(2)}) async-start(bf16[8,64,538]{2,1,0:T(8,128)(2,1)} %bitcast_dynamic-update-slice_fusion), calls=%async_computation | async-start | bytes 1310720 | tf_op jit(solution)/shard_map/all_to_all | solution.py:89
  75.4 9.7 %all-to-all-done = bf16[8,64,538]{2,1,0:T(8,128)(2,1)} async-done(((bf16[8,64,538]{2,1,0:T(8,128)(2,1)}), bf16[8,64,538]{2,1,0:T(8,128)(2,1)}, u32[]{:S(2)}, u32[]{:S(2)}) %all-to-all-start) | async-done | bytes 550944 | tf_op jit(solution)/shard_map/all_to_all | solution.py:89
  85.1 2.3 fusion.6
  87.5 32.9 %all_to_all.42 = f32[8,64,1152]{2,1,0:T(8,128)S(1)} all-to-all(f32[8,64,1152]{2,1,0:T(8,128)S(1)} %fusion.6), channel_id=1, replica_groups=mesh['row_0'=4,'row_1'=2,'col_0'=4,'col_1'=8] {'row_0','row_1'}, dimensions={0} | all-to-all | bytes 4718592 | tf_op jit(solution)/shard_map/all_to_all | solution.py:42
  120.8 1.2 broadcast_in_dim.33
  122.0 4.7 %all-to-all-start.3 = ((bf16[8,64,1152]{2,1,0:T(8,128)(2,1)}), bf16[8,64,1152]{2,1,0:T(8,128)(2,1)S(1)}, u32[]{:S(2)}, u32[]{:S(2)}) async-start(bf16[8,64,1152]{2,1,0:T(8,128)(2,1)} %broadcast_in_dim.33), calls=%async_computation.3 | async-start | bytes 2359296 | tf_op jit(solution)/shard_map/all_to_all | solution.py:27
  128.0 14.5 %all-to-all-done.3 = bf16[8,64,1152]{2,1,0:T(8,128)(2,1)S(1)} async-done(((bf16[8,64,1152]{2,1,0:T(8,128)(2,1)}), bf16[8,64,1152]{2,1,0:T(8,128)(2,1)S(1)}, u32[]{:S(2)}, u32[]{:S(2)}) %all-to-all-start.3) | async-done | bytes 1179680 | tf_op jit(solution)/shard_map/all_to_all | solution.py:27
  142.5 8.2 %fusion.1 = (f32[]{:T(128)}, f32[512,2048]{1,0:T(8,128)S(1)}) fusion(f32[]{:T(128)S(6)} %copy.30, bf16[512,1152]{1,0:T(8,128)(2,1)S(1)} %bitcast.34, bf16[2048,1152]{1,0:T(8,128)(2,1)} %all-gather.2.cloned.1.call-done, f32[]{:T(128)S(6)} %exp.10, s32[2048]{0:T(1024)S(1)} %iota_add_fusion, s32[512]{0:T(512)S(1)} %fusion.21), kind=kOutput, calls=%fused_computation.1 | convolution fusion | flops 2429550592 | bytes 10102796 | tf_op jit(solution)/shard_map/dot_general | solution.py:70
  150.8 3.7 %convolution_multiply_fusion = f32[512,1152]{1,0:T(8,128)S(1)} fusion(bf16[2048,1152]{1,0:T(8,128)(2,1)S(1)} %copy-done.6, f32[512,2048]{1,0:T(8,128)S(1)} %get-tuple-element.15, s32[2048]{0:T(1024)S(1)} %iota_add_fusion, s32[512]{0:T(512)S(1)} %fusion.21, f32[]{:T(128)S(6)} %exp.10), kind=kOutput, calls=%fused_computation.6 | convolution fusion | flops 2425946112 | bytes 11282436 | tf_op jit(solution)/shard_map/dot_general | solution.py:78
  154.5 32.7 %all_to_all.43 = f32[8,64,1152]{2,1,0:T(8,128)S(1)} all-to-all(f32[8,64,1152]{2,1,0:T(8,128)S(1)} %bitcast.33), channel_id=1, replica_groups=mesh['row_0'=4,'row_1'=2,'col_0'=4,'col_1'=8] {'row_0','row_1'}, dimensions={0} | all-to-all | bytes 4718592 | tf_op jit(solution)/shard_map/all_to_all | solution.py:42
  187.8 19.6 %all_to_all.44 = bf16[8,64,1152]{2,1,0:T(8,128)(2,1)S(1)} all-to-all(bf16[8,64,1152]{2,1,0:T(8,128)(2,1)S(1)} %broadcast_in_dim.34), channel_id=1, replica_groups=mesh['row_0'=4,'row_1'=2,'col_0'=4,'col_1'=8] {'row_0','row_1'}, dimensions={0} | all-to-all | bytes 2359296 | tf_op jit(solution)/shard_map/all_to_all | solution.py:27
  207.4 3.8 %convolution_bitcast_fusion = f32[1152,538]{1,0:T(8,128)} fusion(bf16[8,64,1152]{2,1,0:T(8,128)(2,1)S(1)} %all_to_all.44, bf16[8,64,538]{2,1,0:T(8,128)(2,1)} %all-to-all-done), kind=kOutput, calls=%fused_computation.5 | convolution fusion | flops 634650624 | bytes 4209664 | tf_op jit(solution)/shard_map/dot_general | solution.py:125
  211.2 35.5 %reduce-scatter.4.cloned.1.call-done = f32[288,538]{1,0:T(8,128)} async-done(((f32[1152,538]{1,0:T(8,128)}), f32[288,538]{1,0:T(8,128)}) %reduce-scatter.4.cloned.1.call-update) | async-done | bytes 619792 | tf_op jit(solution)/shard_map/reduce_scatter | solution.py:48
  246.7 23.7 %fusion = f32[48,538]{1,0:T(8,128)S(1)} fusion(f32[288,538]{1,0:T(8,128)} %reduce-scatter.4.cloned.1.call-done), kind=kCustom, calls=%all-reduce-scatter | all-reduce-scatter fusion | flops 206593 | bytes 724096
  270.5 2.8 collective-permute-start
  273.3 2.4 collective-permute-start.1
  277.0 1.0 collective-permute-done.1
  278.5 8.5 %all_to_all.45 = f32[8,1,36]{2,1,0:T(1,128)S(1)} all-to-all(f32[8,1,36]{2,1,0:T(1,128)S(1)} %broadcast_in_dim.35), channel_id=1, replica_groups=mesh['row_0'=4,'row_1'=2,'col_0'=4,'col_1'=8] {'row_0','row_1'}, dimensions={0} | all-to-all | bytes 2304 | tf_op jit(solution)/shard_map/all_to_all | solution.py:27
  287.6 10.9 %all-to-all-start.7 = ((f32[32,1,538]{2,1,0:T(1,128)}), f32[32,1,538]{2,1,0:T(1,128)S(1)}, u32[]{:S(2)}, u32[]{:S(2)}) async-start(f32[32,1,538]{2,1,0:T(1,128)} %broadcast_in_dim.36), calls=%async_computation.8 | async-start | bytes 163840 | tf_op jit(solution)/shard_map/all_to_all | solution.py:27
  298.6 10.0 %all-to-all-done.7 = f32[32,1,538]{2,1,0:T(1,128)S(1)} async-done(((f32[32,1,538]{2,1,0:T(1,128)}), f32[32,1,538]{2,1,0:T(1,128)S(1)}, u32[]{:S(2)}, u32[]{:S(2)}) %all-to-all-start.7) | async-done | bytes 68896 | tf_op jit(solution)/shard_map/all_to_all | solution.py:27
  309.4 9.8 %all-reduce.4 = (f32[]{:T(128)}, f32[]{:T(128)}) all-reduce(f32[]{:T(128)} %multiply_reduce_fusion.2, f32[]{:T(128)} %get-tuple-element.14), channel_id=1, replica_groups=mesh['row_0'=4,'row_1'=2,'col_0'=4,'col_1'=8] {'row_0'}, use_global_device_ids=true, to_apply=%region_12.13 | all-reduce | flops 2 | bytes 16 | tf_op jit(solution)/shard_map/psum | solution.py:58
  319.2 3.1 all-reduce.5
  322.3 9.5 %all-reduce.3 = (f32[]{:T(128)}, f32[]{:T(128)}) all-reduce(f32[]{:T(128)} %get-tuple-element.12, f32[]{:T(128)} %get-tuple-element.13), channel_id=1, replica_groups=mesh['row_0'=4,'row_1'=2,'col_0'=4,'col_1'=8] {'col_0'}, use_global_device_ids=true, to_apply=%region_14.15 | all-reduce | flops 2 | bytes 16 | tf_op jit(solution)/shard_map/psum | solution.py:58
  331.8 15.7 %all-reduce.2 = (f32[]{:T(128)}, f32[]{:T(128)}) all-reduce(f32[]{:T(128)} %get-tuple-element.8, f32[]{:T(128)} %get-tuple-element.9), channel_id=1, replica_groups=mesh['row_0'=4,'row_1'=2,'col_0'=4,'col_1'=8] {'col_1'}, use_global_device_ids=true, to_apply=%region_15.16 | all-reduce | flops 2 | bytes 16 | tf_op jit(solution)/shard_map/psum | solution.py:58
  348.2 0.7 fusion.13
  (52 shorter events, 9.3 us)
Async XLA Ops:
  7.2 16.6 %copy-start.1 = (bf16[64,4304]{1,0:T(8,128)(2,1)S(1)}, bf16[64,4304]{1,0:T(8,128)(2,1)}, u32[]{:S(2)}) copy-start(bf16[64,4304]{1,0:T(8,128)(2,1)} %param.9) | copy-start | bytes 1652740
  7.2 135.4 %all-gather.2.cloned.1.call-start = ((), (), s32[]{:S(2)}) async-start(), calls=%async_computation.9 | async-start | bytes 4866048 | tf_op jit(solution)/shard_map/all_gather | solution.py:112
  12.2 57.7 %all-to-all-start.1 = ((bf16[32,36,538]{2,1,0:T(8,128)(2,1)}), bf16[32,36,538]{2,1,0:T(8,128)(2,1)S(1)}, u32[]{:S(2)}, u32[]{:S(2)}) async-start(bf16[32,36,538]{2,1,0:T(8,128)(2,1)} %broadcast_in_dim.32), calls=%async_computation.1 | async-start | bytes 3276800 | tf_op jit(solution)/shard_map/all_to_all | solution.py:27
  69.9 15.2 %all-to-all-start = ((bf16[8,64,538]{2,1,0:T(8,128)(2,1)}), bf16[8,64,538]{2,1,0:T(8,128)(2,1)}, u32[]{:S(2)}, u32[]{:S(2)}) async-start(bf16[8,64,538]{2,1,0:T(8,128)(2,1)} %bitcast_dynamic-update-slice_fusion), calls=%async_computation | async-start | bytes 1310720 | tf_op jit(solution)/shard_map/all_to_all | solution.py:89
  87.4 33.1 %copy-start = (bf16[64,1152]{1,0:T(8,128)(2,1)S(1)}, bf16[64,1152]{1,0:T(8,128)(2,1)}, u32[]{:S(2)}) copy-start(bf16[64,1152]{1,0:T(8,128)(2,1)} %param.8) | copy-start | bytes 442372
  122.0 20.6 %all-to-all-start.3 = ((bf16[8,64,1152]{2,1,0:T(8,128)(2,1)}), bf16[8,64,1152]{2,1,0:T(8,128)(2,1)S(1)}, u32[]{:S(2)}, u32[]{:S(2)}) async-start(bf16[8,64,1152]{2,1,0:T(8,128)(2,1)} %broadcast_in_dim.33), calls=%async_computation.3 | async-start | bytes 2359296 | tf_op jit(solution)/shard_map/all_to_all | solution.py:27
  126.6 120.1 %reduce-scatter.4.cloned.1.call-start = ((), (), s32[]{:S(2)}) async-start(), calls=%async_computation.10 | async-start | bytes 3686400 | tf_op jit(solution)/shard_map/reduce_scatter | solution.py:48
  142.5 8.2 %copy-start.6 = (bf16[2048,1152]{1,0:T(8,128)(2,1)S(1)}, bf16[2048,1152]{1,0:T(8,128)(2,1)}, u32[]{:S(2)}) copy-start(bf16[2048,1152]{1,0:T(8,128)(2,1)} %all-gather.2.cloned.1.call-done) | copy-start | bytes 14155780
  207.4 68.3 %copy-start.5 = (u32[256]{0:T(256)S(1)}, u32[256]{0:T(256)}, u32[]{:S(2)}) copy-start(u32[256]{0:T(256)} %constant.101) | copy-start | bytes 3076
  211.2 87.3 %copy-start.7 = (f32[36]{0:T(128)S(1)}, f32[36]{0:T(128)}, u32[]{:S(2)}) copy-start(f32[36]{0:T(128)} %param.12) | copy-start | bytes 436
  211.2 97.4 %copy-start.3 = (f32[538]{0:T(1024)S(1)}, f32[538]{0:T(1024)}, u32[]{:S(2)}) copy-start(f32[538]{0:T(1024)} %param.13) | copy-start | bytes 6460
  270.5 7.5 %collective-permute-start = (f32[48,538]{1,0:T(8,128)S(1)}, f32[48,538]{1,0:T(8,128)S(1)}, u32[]{:S(2)}, u32[]{:S(2)}) collective-permute-start(f32[48,538]{1,0:T(8,128)S(1)} %fusion), channel_id=1, source_target_pairs={{0,1},{1,2},{2,3},{3,4},{4,5},{5,6},{6,7},{8,9},{9,10},{10,11},{11... | collective-permute-start | bytes 309896
  273.3 4.6 %collective-permute-start.1 = (f32[36,538]{1,0:T(8,128)S(1)}, f32[36,538]{1,0:T(8,128)S(1)}, u32[]{:S(2)}, u32[]{:S(2)}) collective-permute-start(f32[36,538]{1,0:T(8,128)S(1)} %slice), channel_id=1, source_target_pairs={{0,2},{1,3},{2,4},{3,5},{4,6},{5,7},{8,10},{9,11},{10,12},{11,13},... | collective-permute-start | bytes 232424
  287.6 20.9 %all-to-all-start.7 = ((f32[32,1,538]{2,1,0:T(1,128)}), f32[32,1,538]{2,1,0:T(1,128)S(1)}, u32[]{:S(2)}, u32[]{:S(2)}) async-start(f32[32,1,538]{2,1,0:T(1,128)} %broadcast_in_dim.36), calls=%async_computation.8 | async-start | bytes 163840 | tf_op jit(solution)/shard_map/all_to_all | solution.py:27
  298.5 51.0 %copy-start.4 = (f32[36]{0:T(128)}, f32[36]{0:T(128)S(1)}, u32[]{:S(2)}) copy-start(f32[36]{0:T(128)S(1)} %multiply_add_fusion.2) | copy-start | bytes 436
  308.7 40.9 %copy-start.2 = (f32[538]{0:T(1024)}, f32[538]{0:T(1024)S(1)}, u32[]{:S(2)}) copy-start(f32[538]{0:T(1024)S(1)} %multiply_add_fusion.1) | copy-start | bytes 6460
Sparse Core Ops, SparseCore 0:
  10.6 92.2 all-gather.1
  211.4 35.3 reduce-scatter.3
